TPU v7x, 32 devices: a whole 2x2x4 slice. The times are simulated.
32 devices in a mesh: area: 8 (over z, y), tie: 4 (over x, core).
Axes of the slice: x: 2, y: 2, z: 4, core: 2. Of those that a mesh axis runs over, the one named last changes fastest.
Arguments:
- ginv: bfloat16 [128, 1024, 1024], P(('area', 'tie'))
- rhs: float32 [131072, 128], P(('area', 'tie')), may hold values from -6 to 6
- bnd_row: int32 [128, 128], P(('area', 'tie')), may hold values from -1 to 1023, as said below
- bnd_var: int32 [128, 128], P(('area', 'tie')), may hold values from -1 to 2047, as said below
Outputs:
- states: float32 [131072, 128], P(('area', 'tie'))
- consensus: float32 [2048, 128], P(('area', 'tie'))
- dual_value: float32 [16384, 128], P(('area', 'tie'))
Inputs may be any that keep to these rules, and one draw needn't show every extreme that they name: `bnd_row`: -1 marks an unused entry slot; the live rows of one area are distinct. `bnd_var`: -1 exactly where bnd_row is -1. Variable v is owned by the device holding rows v of the consensus output, block v // 64. The areas of one device hold at most 4 live entries owned by any one device; in every draw some owner holds exactly 4 from every device.
All inputs are finite; a program needn't handle non-finite values.
Results may differ from a plain program's by a relative error of at most 0.003.
Values sent between devices are 32-bit elements; how exact they have to be, the bound alone decides.
A program may use at most 64 MiB of HBM per device.

v0:
```python
import jax
import jax.numpy as jnp
from jax import lax
from jax.sharding import PartitionSpec as P

SLOT = 4
VAR_DEV = 64
ITERS = 4


PENALTY = 1.0


def on_device(ginv, rhs, bnd_row, bnd_var):
    area_dev, state_size, _ = ginv.shape
    snap_count = rhs.shape[1]
    bound_size = bnd_row.shape[1]
    entries = area_dev * bound_size
    area_count = lax.axis_size("area")
    tie_count = lax.axis_size("tie")
    device_total = area_count * tie_count
    capacity = device_total * SLOT
    row_flat = bnd_row.reshape(entries)
    var_flat = bnd_var.reshape(entries)
    active = row_flat >= 0
    offsets = jnp.repeat(jnp.arange(area_dev, dtype=jnp.int32) * state_size, bound_size)
    state_row = jnp.where(active, offsets + row_flat, 0)
    owners = jnp.where(active, var_flat // VAR_DEV, device_total)
    onehot = (owners[:, None] == jnp.arange(device_total, dtype=jnp.int32)[None, :]).astype(
        jnp.int32
    )
    placed = jnp.sum(onehot * (jnp.cumsum(onehot, axis=0) - 1), axis=1)
    slot_of_entry = jnp.where(active, owners * SLOT + placed, capacity)
    entry_of_slot = jnp.full((capacity + 1,), entries, jnp.int32)
    entry_of_slot = entry_of_slot.at[slot_of_entry].set(jnp.arange(entries, dtype=jnp.int32))[
        :capacity
    ]
    local_var = jnp.where(active, var_flat % VAR_DEV, -1)
    slot_var = jnp.concatenate([local_var, jnp.full((1,), -1, jnp.int32)])[entry_of_slot]
    recv_var = lax.all_to_all(
        slot_var.reshape(device_total, SLOT),
        ("area", "tie"),
        split_axis=0,
        concat_axis=0,
        tiled=True,
    ).reshape(capacity)
    member = (recv_var[None, :] == jnp.arange(VAR_DEV, dtype=jnp.int32)[:, None]).astype(
        jnp.float32
    )
    counts = jnp.sum(member, axis=1)
    inverse = 1.0 / jnp.maximum(counts, 1.0)
    mask = active[:, None]
    zero_row = jnp.zeros((1, snap_count), jnp.float32)
    dual_value = jnp.zeros((entries, snap_count), jnp.float32)
    agreed = jnp.zeros((entries, snap_count), jnp.float32)
    states = None
    consensus = None
    for iteration in range(ITERS):
        shifted = jnp.where(mask, agreed - dual_value, 0.0)
        update = (
            jnp.zeros((area_dev * state_size, snap_count), jnp.float32).at[state_row].add(shifted)
        )
        blended = (
            (rhs + PENALTY * update).astype(jnp.bfloat16).reshape(area_dev, state_size, snap_count)
        )
        states = jnp.einsum("aij,ajs->ais", ginv, blended, preferred_element_type=jnp.float32)
        states = states.reshape(area_dev * state_size, snap_count)
        local_part = jnp.where(mask, states[state_row] + dual_value, 0.0)
        outgoing = jnp.concatenate([local_part, zero_row])[entry_of_slot]
        incoming = lax.all_to_all(
            outgoing.reshape(device_total, SLOT, snap_count),
            ("area", "tie"),
            split_axis=0,
            concat_axis=0,
            tiled=True,
        )
        incoming = incoming.reshape(capacity, snap_count)
        totals = jnp.dot(member, incoming, precision=lax.Precision.HIGHEST)
        consensus = totals * inverse[:, None]
        returning = jnp.dot(member.T, consensus, precision=lax.Precision.HIGHEST)
        returned = lax.all_to_all(
            returning.reshape(device_total, SLOT, snap_count),
            ("area", "tie"),
            split_axis=0,
            concat_axis=0,
            tiled=True,
        )
        returned = returned.reshape(capacity, snap_count)
        agreed = jnp.concatenate([returned, zero_row])[slot_of_entry]
        agreed = jnp.where(mask, agreed, 0.0)
        dual_value = jnp.where(mask, local_part - agreed, 0.0)
    return (states, consensus, dual_value)


def solution(mesh):
    in_specs = (
        P(("area", "tie"), None, None),
        P(("area", "tie"), None),
        P(("area", "tie"), None),
        P(("area", "tie"), None),
    )
    out_specs = (P(("area", "tie"), None), P(("area", "tie"), None), P(("area", "tie"), None))
    return jax.shard_map(
        on_device, mesh=mesh, in_specs=in_specs, out_specs=out_specs, check_vma=False
    )
```

profile of v0, /device:TPU:0, one launch (start us, length us, event | category | flops | bytes accessed | tf_op | source)
XLA Modules:
  0.0 169.3 jit_solution(9470250031202733415)
XLA Ops:
  0.7 1.6 copy.65
  2.3 1.2 reduce-window.6
  3.5 0.2 slice_reduce_fusion
  3.8 0.1 fusion.21
  4.0 2.4 %scatter_custom_fusion = s32[129]{0:T(256)S(1)} fusion(s32[512]{0:T(512)S(1)} %bitcast.149, s32[512]{0:T(512)S(1)} %iota.19, s32[]{:T(128)} %constant.53.clone.1), kind=kCustom, calls=%fused_computation.115 | custom fusion | bytes 520 | tf_op jit(solution)/shard_map/scatter | solution.py:35
  6.5 1.0 gather_fusion
  7.4 0.7 all_to_all.30
  8.2 7.3 %all-to-all-start = ((s32[32,1,4]{2,1,0:T(1,128)}), s32[32,1,4]{2,1,0:T(1,128)S(1)}, u32[]{:S(2)}, u32[]{:S(2)}) async-start(s32[32,1,4]{2,1,0:T(1,128)} %bitcast.8), calls=%async_computation | async-start | bytes 32768 | tf_op jit(solution)/shard_map/all_to_all | solution.py:40
  15.5 1.3 copy.61
  16.8 1.4 copy.62
  18.1 1.3 copy.63
  19.5 4.3 %scatter_custom_fusion.1 = f32[4096,128]{1,0:T(8,128)S(1)} fusion(f32[4096,128]{1,0:T(8,128)S(1)} %copy.65, s32[512]{0:T(512)S(1)} %bitcast.145, f32[]{:T(128)} %constant.61.clone.1), kind=kCustom, calls=%fused_computation.49 | custom fusion | flops 65536 | bytes 2097156 | tf_op jit(solution)/shard_map/scatter-add | solution.py:61
  23.8 0.1 convert_element_type.21
  23.9 7.6 %convolution_bitcast_fusion.3 = f32[4,1024,128]{1,2,0:T(8,128)} fusion(bf16[4,1024,128]{2,1,0:T(8,128)(2,1)S(1)} %bitcast.116, bf16[4,1024,1024]{2,1,0:T(8,128)(2,1)} %param.4), kind=kOutput, calls=%fused_computation.21 | convolution fusion | flops 1073741824 | bytes 11534336 | tf_op jit(solution)/shard_map/aij,ajs->ais/dot_general | solution.py:66
  31.5 1.9 %copy.33 = f32[4,1024,128]{2,1,0:T(8,128)S(1)} copy(f32[4,1024,128]{1,2,0:T(8,128)} %convolution_bitcast_fusion.3) | data formatting | bytes 4194304 | tf_op jit(solution)/shard_map/aij,ajs->ais/dot_general | solution.py:66
  33.4 1.0 gather_fusion.1
  34.4 0.1 broadcast_select_fusion
  34.6 1.2 gather_fusion.2
  35.9 5.8 %all-to-all-start.1 = ((f32[32,4,128]{2,1,0:T(4,128)}), f32[32,4,128]{2,1,0:T(4,128)S(1)}, u32[]{:S(2)}, u32[]{:S(2)}) async-start(f32[32,4,128]{2,1,0:T(4,128)} %bitcast.12), calls=%async_computation.1 | async-start | bytes 131072 | tf_op jit(solution)/shard_map/all_to_all | solution.py:70
  41.7 0.5 broadcast.340
  42.2 0.7 reduce.5
  43.0 0.1 convert_reduce_fusion
  43.1 6.0 %all-to-all-done.1 = f32[32,4,128]{2,1,0:T(4,128)S(1)} async-done(((f32[32,4,128]{2,1,0:T(4,128)}), f32[32,4,128]{2,1,0:T(4,128)S(1)}, u32[]{:S(2)}, u32[]{:S(2)}) %all-to-all-start.1) | async-done | bytes 65568 | tf_op jit(solution)/shard_map/all_to_all | solution.py:70
  49.1 0.2 convolution_multiply_fusion.3
  49.3 0.9 fusion.26
  50.2 2.6 %all-to-all-start.2 = ((f32[32,4,128]{2,1,0:T(4,128)}), f32[32,4,128]{2,1,0:T(4,128)S(1)}, u32[]{:S(2)}, u32[]{:S(2)}) async-start(f32[32,4,128]{2,1,0:T(4,128)} %bitcast.14), calls=%async_computation.2 | async-start | bytes 131072 | tf_op jit(solution)/shard_map/all_to_all | solution.py:81
  52.8 7.4 %all-to-all-done.2 = f32[32,4,128]{2,1,0:T(4,128)S(1)} async-done(((f32[32,4,128]{2,1,0:T(4,128)}), f32[32,4,128]{2,1,0:T(4,128)S(1)}, u32[]{:S(2)}, u32[]{:S(2)}) %all-to-all-start.2) | async-done | bytes 65568 | tf_op jit(solution)/shard_map/all_to_all | solution.py:81
  60.2 1.0 gather_fusion.3
  61.2 4.6 %scatter_custom_fusion.2 = f32[4096,128]{1,0:T(8,128)S(1)} fusion(f32[4096,128]{1,0:T(8,128)S(1)} %copy-done.2, s32[512]{0:T(512)S(1)} %bitcast.146, f32[512,128]{1,0:T(8,128)S(1)} %gather_fusion.3, f32[]{:T(128)} %constant.61.clone.1, pred[512]{0:T(512)(128)(4,1)S(1)} %bitcast.136, f32[512,128]{1,0:T(8,128)S(1)} %gather_fusion.1), kind=kCustom, calls=%fused_computation.38 | custom fusion | flops 458752 | bytes 2621956 | tf_op jit(solution)/shard_map/scatter-add | solution.py:61
  65.9 7.6 %convolution_bitcast_fusion.2 = f32[4,1024,128]{1,2,0:T(8,128)} fusion(bf16[4,1024,128]{2,1,0:T(8,128)(2,1)S(1)} %bitcast.117, bf16[4,1024,1024]{2,1,0:T(8,128)(2,1)} %param.4), kind=kOutput, calls=%fused_computation.20 | convolution fusion | flops 1073741824 | bytes 11534336 | tf_op jit(solution)/shard_map/aij,ajs->ais/dot_general | solution.py:66
  73.5 1.9 %copy.35 = f32[4,1024,128]{2,1,0:T(8,128)S(1)} copy(f32[4,1024,128]{1,2,0:T(8,128)} %convolution_bitcast_fusion.2) | data formatting | bytes 4194304 | tf_op jit(solution)/shard_map/aij,ajs->ais/dot_general | solution.py:66
  75.4 1.0 gather_fusion.4
  76.5 0.1 add_select_fusion.2
  76.6 0.6 gather_fusion.5
  77.3 9.1 %all_to_all.49 = f32[32,4,128]{2,1,0:T(4,128)S(1)} all-to-all(f32[32,4,128]{2,1,0:T(4,128)S(1)} %bitcast.132), channel_id=1, replica_groups=mesh['area'=8,'tie'=4] {'area','tie'}, dimensions={0} | all-to-all | bytes 131072 | tf_op jit(solution)/shard_map/all_to_all | solution.py:70
  86.4 0.2 convolution_multiply_fusion.2
  86.6 0.3 fusion.25
  86.8 9.1 %all_to_all.50 = f32[32,4,128]{2,1,0:T(4,128)S(1)} all-to-all(f32[32,4,128]{2,1,0:T(4,128)S(1)} %bitcast.125), channel_id=1, replica_groups=mesh['area'=8,'tie'=4] {'area','tie'}, dimensions={0} | all-to-all | bytes 131072 | tf_op jit(solution)/shard_map/all_to_all | solution.py:81
  95.9 1.0 gather_fusion.6
  97.0 4.4 %scatter_custom_fusion.3 = f32[4096,128]{1,0:T(8,128)S(1)} fusion(f32[4096,128]{1,0:T(8,128)S(1)} %copy-done.1, s32[512]{0:T(512)S(1)} %bitcast.147, f32[512,128]{1,0:T(8,128)S(1)} %gather_fusion.6, f32[512,128]{1,0:T(8,128)S(1)} %add_select_fusion.2, f32[]{:T(128)} %constant.61.clone.1, pred[512]{0:T(512)(128)(4,1)S(1)} %bitcast.138), kind=kCustom, calls=%fused_computation.33 | custom fusion | flops 393216 | bytes 2621956 | tf_op jit(solution)/shard_map/scatter-add | solution.py:61
  101.4 0.1 convert_element_type.24
  101.5 7.6 %convolution_bitcast_fusion.1 = f32[4,1024,128]{1,2,0:T(8,128)} fusion(bf16[4,1024,128]{2,1,0:T(8,128)(2,1)S(1)} %bitcast.118, bf16[4,1024,1024]{2,1,0:T(8,128)(2,1)} %param.4), kind=kOutput, calls=%fused_computation.19 | convolution fusion | flops 1073741824 | bytes 11534336 | tf_op jit(solution)/shard_map/aij,ajs->ais/dot_general | solution.py:66
  109.1 1.9 %copy.37 = f32[4,1024,128]{2,1,0:T(8,128)S(1)} copy(f32[4,1024,128]{1,2,0:T(8,128)} %convolution_bitcast_fusion.1) | data formatting | bytes 4194304 | tf_op jit(solution)/shard_map/aij,ajs->ais/dot_general | solution.py:66
  111.1 1.0 gather_fusion.7
  112.1 0.1 add_select_fusion.1
  112.3 0.6 gather_fusion.8
  112.9 9.1 %all_to_all.51 = f32[32,4,128]{2,1,0:T(4,128)S(1)} all-to-all(f32[32,4,128]{2,1,0:T(4,128)S(1)} %bitcast.133), channel_id=1, replica_groups=mesh['area'=8,'tie'=4] {'area','tie'}, dimensions={0} | all-to-all | bytes 131072 | tf_op jit(solution)/shard_map/all_to_all | solution.py:70
  122.0 0.2 convolution_multiply_fusion.1
  122.2 0.3 fusion.24
  122.5 9.1 %all_to_all.52 = f32[32,4,128]{2,1,0:T(4,128)S(1)} all-to-all(f32[32,4,128]{2,1,0:T(4,128)S(1)} %bitcast.128), channel_id=1, replica_groups=mesh['area'=8,'tie'=4] {'area','tie'}, dimensions={0} | all-to-all | bytes 131072 | tf_op jit(solution)/shard_map/all_to_all | solution.py:81
  131.6 1.0 gather_fusion.9
  132.6 4.6 %scatter_custom_fusion.4 = f32[4096,128]{1,0:T(8,128)S(1)} fusion(f32[4096,128]{1,0:T(8,128)S(1)} %copy-done, s32[512]{0:T(512)S(1)} %bitcast.148, f32[512,128]{1,0:T(8,128)S(1)} %gather_fusion.9, f32[512,128]{1,0:T(8,128)S(1)} %add_select_fusion.1, f32[]{:T(128)} %constant.61.clone.1, pred[512]{0:T(512)(128)(4,1)S(1)} %bitcast.140), kind=kCustom, calls=%fused_computation.28 | custom fusion | flops 393216 | bytes 2621956 | tf_op jit(solution)/shard_map/scatter-add | solution.py:61
  137.2 0.1 convert_element_type.25
  137.4 7.6 %convolution_bitcast_fusion = f32[4,1024,128]{1,2,0:T(8,128)} fusion(bf16[4,1024,128]{2,1,0:T(8,128)(2,1)S(1)} %bitcast.119, bf16[4,1024,1024]{2,1,0:T(8,128)(2,1)} %param.4), kind=kOutput, calls=%fused_computation.18 | convolution fusion | flops 1073741824 | bytes 11534336 | tf_op jit(solution)/shard_map/aij,ajs->ais/dot_general | solution.py:66
  145.0 1.9 %copy.39 = f32[4,1024,128]{2,1,0:T(8,128)S(1)} copy(f32[4,1024,128]{1,2,0:T(8,128)} %convolution_bitcast_fusion) | data formatting | bytes 4194304 | tf_op jit(solution)/shard_map/aij,ajs->ais/dot_general | solution.py:66
  146.9 1.0 gather_fusion.10
  147.9 0.1 add_select_fusion
  148.1 0.6 gather_fusion.11
  148.8 9.1 %all_to_all.53 = f32[32,4,128]{2,1,0:T(4,128)S(1)} all-to-all(f32[32,4,128]{2,1,0:T(4,128)S(1)} %bitcast.131), channel_id=1, replica_groups=mesh['area'=8,'tie'=4] {'area','tie'}, dimensions={0} | all-to-all | bytes 131072 | tf_op jit(solution)/shard_map/all_to_all | solution.py:70
  157.9 0.2 convolution_multiply_fusion
  158.0 0.3 fusion.23
  158.3 9.1 %all_to_all.54 = f32[32,4,128]{2,1,0:T(4,128)S(1)} all-to-all(f32[32,4,128]{2,1,0:T(4,128)S(1)} %bitcast.130), channel_id=1, replica_groups=mesh['area'=8,'tie'=4] {'area','tie'}, dimensions={0} | all-to-all | bytes 131072 | tf_op jit(solution)/shard_map/all_to_all | solution.py:81
  167.4 1.0 gather_fusion.12
  168.5 0.8 subtract_select_fusion
  (41 shorter events, 0.6 us)
Async XLA Ops:
  0.6 1.6 copy-start.6
  0.6 1.6 copy-start.5
  8.2 27.7 %all-to-all-start = ((s32[32,1,4]{2,1,0:T(1,128)}), s32[32,1,4]{2,1,0:T(1,128)S(1)}, u32[]{:S(2)}, u32[]{:S(2)}) async-start(s32[32,1,4]{2,1,0:T(1,128)} %bitcast.8), calls=%async_computation | async-start | bytes 32768 | tf_op jit(solution)/shard_map/all_to_all | solution.py:40
  34.6 26.6 %copy-start.2 = (f32[4096,128]{1,0:T(8,128)S(1)}, f32[4096,128]{1,0:T(8,128)}, u32[]{:S(2)}) copy-start(f32[4096,128]{1,0:T(8,128)} %copy.61) | copy-start | bytes 6291460
  35.9 13.3 %all-to-all-start.1 = ((f32[32,4,128]{2,1,0:T(4,128)}), f32[32,4,128]{2,1,0:T(4,128)S(1)}, u32[]{:S(2)}, u32[]{:S(2)}) async-start(f32[32,4,128]{2,1,0:T(4,128)} %bitcast.12), calls=%async_computation.1 | async-start | bytes 131072 | tf_op jit(solution)/shard_map/all_to_all | solution.py:70
  50.2 10.0 %all-to-all-start.2 = ((f32[32,4,128]{2,1,0:T(4,128)}), f32[32,4,128]{2,1,0:T(4,128)S(1)}, u32[]{:S(2)}, u32[]{:S(2)}) async-start(f32[32,4,128]{2,1,0:T(4,128)} %bitcast.14), calls=%async_computation.2 | async-start | bytes 131072 | tf_op jit(solution)/shard_map/all_to_all | solution.py:81
  76.6 20.4 %copy-start.1 = (f32[4096,128]{1,0:T(8,128)S(1)}, f32[4096,128]{1,0:T(8,128)}, u32[]{:S(2)}) copy-start(f32[4096,128]{1,0:T(8,128)} %copy.62) | copy-start | bytes 6291460
  112.2 20.4 %copy-start = (f32[4096,128]{1,0:T(8,128)S(1)}, f32[4096,128]{1,0:T(8,128)}, u32[]{:S(2)}) copy-start(f32[4096,128]{1,0:T(8,128)} %copy.63) | copy-start | bytes 6291460
  146.9 1.9 %copy-start.3 = (f32[4,1024,128]{2,1,0:T(8,128)}, f32[4,1024,128]{2,1,0:T(8,128)S(1)}, u32[]{:S(2)}) copy-start(f32[4,1024,128]{2,1,0:T(8,128)S(1)} %copy.39) | copy-start | bytes 6291460
  158.0 11.3 %copy-start.4 = (f32[64,128]{1,0:T(8,128)}, f32[64,128]{1,0:T(8,128)S(1)}, u32[]{:S(2)}) copy-start(f32[64,128]{1,0:T(8,128)S(1)} %convolution_multiply_fusion) | copy-start | bytes 98308
where the time goes:
time: 170 us; the launch traced here: 169 us
  blocking collectives  54.6 us (32%)
  matrix products  32.7 us (19%)
  local copies, waits for them, and re-layouts  29.7 us (17%)
  other arithmetic  22 us (13%)
  starting transfers between devices  15.7 us (9%)
  waiting for transfers between devices  13.4 us (8%)
    dot_general x4, matrix products, on_device(): jnp.einsum('aij,ajs->ais', ginv, blended, preferred_element_type=jnp.floa...  30.4 us
    all_to_all x3, blocking collectives, on_device(): lax.all_to_all(returning.reshape(device_total, SLOT, snap_count), ('area'...  27.3 us
    all_to_all x3, blocking collectives, on_device(): lax.all_to_all(outgoing.reshape(device_total, SLOT, snap_count), ('area',...  27.3 us
    scatter-add x4, other arithmetic, on_device(): jnp.zeros((area_dev * state_size, snap_count), jnp.float32).at[state_row]  17.9 us
    dot_general x4, local copies, waits for them, and re-layouts, on_device(): jnp.einsum('aij,ajs->ais', ginv, blended, preferred_element_type=jnp.floa...  7.62 us
    all_to_all x1, waiting for transfers between devices, on_device(): lax.all_to_all(returning.reshape(device_total, SLOT, snap_count), ('area'...  7.4 us
    all_to_all x1, starting transfers between devices, on_device(): lax.all_to_all(slot_var.reshape(device_total, SLOT), ('area', 'tie'), spl...  7.33 us
    all_to_all x1, waiting for transfers between devices, on_device(): lax.all_to_all(outgoing.reshape(device_total, SLOT, snap_count), ('area',...  5.97 us
  transfers between devices with their start and end apart: 3, of which 2 were waited for; matrix products, arithmetic and copies ran while one was open for 13% of the time, Pallas kernels for 0%

commit v1 on v0

v1 whole, which is shorter than its diff:
```python
import functools

import jax
import jax.numpy as jnp
from jax import lax
from jax.experimental import pallas as pl
from jax.experimental.pallas import tpu as pltpu
from jax.sharding import PartitionSpec as P

SLOT = 4
VAR_DEV = 64
ITERS = 4
PENALTY = 1.0

MESH = pl.DeviceIdType.MESH
F32 = jnp.float32
BF16 = jnp.bfloat16


def mm(a, b):
    return jnp.dot(a, b, preferred_element_type=F32)


def dot_dims(a, b, da, db):
    return lax.dot_general(a, b, (((da,), (db,)), ((), ())), preferred_element_type=F32)


def parts(x):
    high = x.astype(BF16)
    rest = x - high.astype(F32)
    mid = rest.astype(BF16)
    low = (rest - mid.astype(F32)).astype(BF16)
    return high, mid, low


def mm_parts(onehot, x):
    high, mid, low = parts(x)
    return mm(onehot, high) + (mm(onehot, mid) + mm(onehot, low))


def kernel(
    area_n,
    tie_n,
    srow_col,
    srow_lane,
    svar_col,
    g_hbm,
    rhs_hbm,
    states_ref,
    cons_ref,
    dual_ref,
    g_ref,
    rhs_ref,
    pick,
    out_buf,
    in_buf,
    rhs_b,
    y_base,
    g_bb,
    load_sem,
    send_sem,
    recv_sem,
):
    devices = area_n * tie_n
    area_dev, state_size, _ = g_ref.shape
    cap = devices * SLOT
    snap = dual_ref.shape[1]
    me_a, me_t = lax.axis_index("area"), lax.axis_index("tie")
    me = me_a * tie_n + me_t

    def peer_of(k):
        peer = lax.rem(me + k, devices)
        return peer, (peer // tie_n, lax.rem(peer, tie_n))

    barrier = pltpu.get_barrier_semaphore()

    @pl.loop(1, devices)
    def _(k):
        _, device = peer_of(k)
        pl.semaphore_signal(barrier, inc=1, device_id=device, device_id_type=MESH)

    def g_load(a):
        return pltpu.make_async_copy(g_hbm.at[a], g_ref.at[a], load_sem.at[0, a])

    def rhs_load(a):
        return pltpu.make_async_copy(rhs_hbm.at[a], rhs_ref.at[a], load_sem.at[1, a])

    for a in range(area_dev):
        g_load(a).start()
        rhs_load(a).start()

    def send(phase, value):
        out_buf[phase] = value.reshape(devices, SLOT, snap)
        in_buf[phase, me] = out_buf[phase, me]

        @pl.loop(1, devices)
        def _(k):
            peer, device = peer_of(k)
            pltpu.make_async_remote_copy(
                src_ref=out_buf.at[phase, peer],
                dst_ref=in_buf.at[phase, me],
                send_sem=send_sem.at[phase],
                recv_sem=recv_sem.at[phase],
                device_id=device,
                device_id_type=MESH,
            ).start()

    def receive(phase):
        span = in_buf.at[phase, pl.ds(0, devices - 1)]
        pltpu.make_async_copy(span, span, recv_sem.at[phase]).wait()
        return in_buf[phase].reshape(cap, snap)

    lane = lax.broadcasted_iota(jnp.int32, (cap, snap), 1)
    member_out = (svar_col[...] == lane).astype(F32)
    pl.semaphore_wait(barrier, devices - 1)
    send(0, member_out)

    rhs_b[...] = jnp.zeros_like(rhs_b)
    y_base[...] = jnp.zeros_like(y_base)
    g_bb[...] = jnp.zeros_like(g_bb)

    @pl.loop(0, area_dev)
    def _(a):
        column = lax.broadcasted_iota(jnp.int32, (cap, state_size), 1) + a * state_size
        chosen = (jnp.broadcast_to(srow_col[:, :1], (cap, state_size)) == column).astype(F32)
        chosen = chosen.astype(BF16)
        line = lax.broadcasted_iota(jnp.int32, (state_size, cap), 0) + a * state_size
        pick[a] = (
            (jnp.broadcast_to(srow_lane[:1, :], (state_size, cap)) == line)
            .astype(F32)
            .astype(BF16)
        )
        rhs_load(a).wait()
        high, mid, low = parts(rhs_ref[a])
        rhs_b[...] += mm(chosen, high) + (mm(chosen, mid) + mm(chosen, low))
        g_load(a).wait()
        rows = mm(chosen, g_ref[a]).astype(BF16)
        y_base[...] += mm(rows, high)
        g_bb[...] += mm(rows, pick[a])

    inner = g_bb[...].astype(BF16)
    own = rhs_b[...]
    first = y_base[...]
    steady = first - mm(inner, own.astype(BF16))

    member = receive(0).astype(BF16)
    same = dot_dims(member, member, 1, 1)
    share = 1.0 / jnp.maximum(jnp.sum(same, axis=1, keepdims=True), 1.0)
    same = same.astype(BF16)
    dual = jnp.zeros((cap, snap), F32)
    update = jnp.zeros((cap, snap), F32)
    for it in range(ITERS):
        if it == 0:
            local = first
        else:
            blended = (own + PENALTY * update).astype(BF16)
            local = steady + mm(inner, blended) + dual
        send(1 + 2 * it, local)
        if it == ITERS - 1:
            moved = parts(update)

            @pl.loop(0, area_dev)
            def _(a):
                scattered = mm(pick[a], moved[0]) + (mm(pick[a], moved[1]) + mm(pick[a], moved[2]))
                mixed = (rhs_ref[a] + PENALTY * scattered).astype(BF16)
                states_ref[a] = mm(g_ref[a], mixed)

        incoming = receive(1 + 2 * it)
        send(2 + 2 * it, mm_parts(same, incoming) * share)
        if it == ITERS - 1:
            high, mid, low = parts(incoming)
            totals = dot_dims(member, high, 0, 0) + (
                dot_dims(member, mid, 0, 0) + dot_dims(member, low, 0, 0)
            )
            counts = dot_dims(member, jnp.ones((cap, snap), BF16), 0, 0)
            consensus = totals * (1.0 / jnp.maximum(counts, 1.0))
            cons_ref[...] = consensus[: cons_ref.shape[0]]
        agreed = receive(2 + 2 * it)
        dual = local - agreed
        update = agreed - dual
    dual_ref[...] = dual

    for phase in range(1 + 2 * ITERS):
        span = out_buf.at[phase, pl.ds(0, devices - 1)]
        pltpu.make_async_copy(span, span, send_sem.at[phase]).wait()


def on_device(ginv, rhs, bnd_row, bnd_var):
    area_dev, state_size, _ = ginv.shape
    snap = rhs.shape[1]
    bound_size = bnd_row.shape[1]
    entries = area_dev * bound_size
    area_n = lax.axis_size("area")
    tie_n = lax.axis_size("tie")
    devices = area_n * tie_n
    cap = devices * SLOT
    row_flat = bnd_row.reshape(entries)
    var_flat = bnd_var.reshape(entries)
    active = row_flat >= 0
    order = jnp.arange(entries, dtype=jnp.int32)
    state_row = (order // bound_size) * state_size + row_flat
    owners = jnp.where(active, var_flat // VAR_DEV, devices)
    owned = owners[:, None] == jnp.arange(devices, dtype=jnp.int32)[None, :]
    earlier = (order[:, None] > order[None, :]).astype(BF16)
    before = mm(earlier, owned.astype(BF16))
    placed = jnp.sum(jnp.where(owned, before, 0.0), axis=1).astype(jnp.int32)
    slot = jnp.where(active, owners * SLOT + placed, -1)
    slots = jnp.arange(cap, dtype=jnp.int32)
    held = slots[:, None] == slot[None, :]
    srow = jnp.sum(jnp.where(held, (state_row + 1)[None, :], 0), axis=1) - 1
    svar = jnp.sum(jnp.where(held, (var_flat % VAR_DEV + 1)[None, :], 0), axis=1) - 1
    phases = 1 + 2 * ITERS
    vmem = pl.BlockSpec(memory_space=pltpu.VMEM)
    hbm = pl.BlockSpec(memory_space=pl.ANY)
    states, consensus, dual = pl.pallas_call(
        functools.partial(kernel, area_n, tie_n),
        out_shape=(
            jax.ShapeDtypeStruct((area_dev, state_size, snap), F32),
            jax.ShapeDtypeStruct((VAR_DEV, snap), F32),
            jax.ShapeDtypeStruct((cap, snap), F32),
        ),
        in_specs=[vmem, vmem, vmem, hbm, hbm],
        out_specs=(vmem, vmem, vmem),
        scratch_shapes=[
            pltpu.VMEM(ginv.shape, BF16),
            pltpu.VMEM((area_dev, state_size, snap), F32),
            pltpu.VMEM((area_dev, state_size, cap), BF16),
            pltpu.VMEM((phases, devices, SLOT, snap), F32),
            pltpu.VMEM((phases, devices, SLOT, snap), F32),
            pltpu.VMEM((cap, snap), F32),
            pltpu.VMEM((cap, snap), F32),
            pltpu.VMEM((cap, cap), F32),
            pltpu.SemaphoreType.DMA((2, area_dev)),
            pltpu.SemaphoreType.DMA((phases,)),
            pltpu.SemaphoreType.DMA((phases,)),
        ],
        compiler_params=pltpu.CompilerParams(
            collective_id=0, has_side_effects=True, vmem_limit_bytes=48 * 1024 * 1024
        ),
        name="admm",
    )(
        jnp.broadcast_to(srow[:, None], (cap, snap)),
        jnp.broadcast_to(srow[None, :], (8, cap)),
        jnp.broadcast_to(svar[:, None], (cap, snap)),
        ginv,
        rhs.reshape(area_dev, state_size, snap),
    )
    spread = (slot[:, None] == slots[None, :]).astype(F32)
    dual = jnp.dot(spread, dual, precision=lax.Precision.HIGHEST)
    return (states.reshape(area_dev * state_size, snap), consensus, dual)


def solution(mesh):
    both = ("area", "tie")
    in_specs = (P(both, None, None), P(both, None), P(both, None), P(both, None))
    out_specs = (P(both, None), P(both, None), P(both, None))
    return jax.shard_map(
        on_device, mesh=mesh, in_specs=in_specs, out_specs=out_specs, check_vma=False
    )
```

time: 170 us -> 58.8 us (0.35)
  blocking collectives: 54.6 us -> 0 us
  Pallas kernels: 0 us -> 52.1 us
  matrix products: 32.7 us -> 1.3 us
  local copies, waits for them, and re-layouts: 29.7 us -> 3.69 us
  other arithmetic: 22 us -> 0.85 us
  starting transfers between devices: 15.7 us -> 0 us
  waiting for transfers between devices: 13.4 us -> 0 us
    all_to_all x6 -> x0, blocking collectives: 54.6 us -> none  [the longest x3 27.3 us: on_device(): lax.all_to_all(returning.reshape(device_total, SLOT, snap_count), ('area'...]
    pallas_call x0 -> x1, Pallas kernels: none -> 52.1 us  [on_device(): pl.pallas_call(functools.partial(kernel, area_n, tie_n), out_shape=(jax.S...]
    dot_general x12 -> x2, matrix products: 32.7 us -> 1.3 us  [the longest x1 1.03 us: on_device(): dual = jnp.dot(spread, dual, precision=lax.Precision.HIGHEST)]
    scatter-add x4 -> x0, other arithmetic: 17.9 us -> none  [on_device(): jnp.zeros((area_dev * state_size, snap_count), jnp.float32).at[state_row]]
    all_to_all x3 -> x0, starting transfers between devices: 15.7 us -> none  [the longest x1 7.33 us: on_device(): lax.all_to_all(slot_var.reshape(device_total, SLOT), ('area', 'tie'), spl...]
    all_to_all x3 -> x0, waiting for transfers between devices: 13.4 us -> none  [the longest x1 7.4 us: on_device(): lax.all_to_all(returning.reshape(device_total, SLOT, snap_count), ('area'...]
    gather x13 -> x0, local copies, waits for them, and re-layouts: 12.4 us -> none  [the longest x4 4.15 us: on_device(): local_part = jnp.where(mask, states[state_row] + dual_value, 0.0)]
    dot_general x4 -> x0, local copies, waits for them, and re-layouts: 7.62 us -> none  [on_device(): jnp.einsum('aij,ajs->ais', ginv, blended, preferred_element_type=jnp.floa...]
  transfers between devices with their start and end apart: 3 -> 0, of which waited for: 2 -> 0; matrix products, arithmetic and copies ran while one was open for 13% -> 0% of each run, Pallas kernels for 0% -> 0%
where the time goes in v1:
time: 58.8 us; the launch traced here: 58.6 us
  Pallas kernels  52.1 us (89%)
  local copies, waits for them, and re-layouts  3.69 us (6%)
  matrix products  1.3 us (2%)
  other arithmetic  0.85 us (1%)
  between operations  0.67 us (1%)
    pallas_call x1, Pallas kernels, on_device(): pl.pallas_call(functools.partial(kernel, area_n, tie_n), out_shape=(jax.S...  52.1 us
    unnamed x4, local copies, waits for them, and re-layouts  3.53 us

profile of v1, /device:TPU:0, one launch (start us, length us, event | category | flops | bytes accessed | tf_op | source)
XLA Modules:
  0.0 58.6 jit_solution(214172999055125963)
XLA Ops:
  0.6 0.7 %fusion.4 = (s32[512]{0:T(512)S(1)}, pred[512]{0:T(512)(128)(4,1)S(1)}, s32[512]{0:T(512)S(1)}, s32[512]{0:T(512)S(1)}) fusion(s32[4,128]{1,0:T(4,128)} %param.7, s32[4,128]{1,0:T(4,128)} %param.6), kind=kLoop, calls=%fused_computation.20 | loop fusion | flops 16896 | bytes 10752 | tf_op jit(solution)/shard_map/jit(_where)/select_n | solution.py:202
  1.3 0.3 fusion
  1.6 0.1 select_reduce_fusion
  1.8 0.1 broadcast_in_dim.59.srow_col
  1.9 0.1 broadcast_in_dim.62.svar_col
  1.9 0.0 copy-start
  1.9 1.6 %copy-done = f32[4096,128]{1,0:T(8,128)S(1)} copy-done((f32[4096,128]{1,0:T(8,128)S(1)}, f32[4096,128]{1,0:T(8,128)}, u32[]{:S(2)}) %copy-start) | copy-done | bytes 2097176
  3.5 52.1 %admm.1 = (f32[4,1024,128]{2,1,0:T(8,128)S(1)}, f32[64,128]{1,0:T(8,128)S(1)}, f32[128,128]{1,0:T(8,128)S(1)}) custom-call(s32[128,128]{1,0:T(8,128)S(1)} %broadcast_in_dim.59.srow_col, s32[8,128]{1,0:T(8,128)S(1)} %broadcast_in_dim.60.srow_lane, s32[128,128]{1,0:T(8,128)S(1)} %broadcast_in_dim.62.svar_col, bf16[4,1024,1024]{2,1,0:T(8,128)(2,1)} %g_hbm.1, ...), custom_call_target="tpu_custom_call" | custom-call | tf_op jit(solution)/shard_map/admm/pallas_call | solution.py:215
  55.7 1.0 %fusion.1 = f32[512,128]{1,0:T(8,128)} fusion(f32[128,128]{1,0:T(8,128)S(1)} %get-tuple-element.8, s32[512]{0:T(512)S(1)} %add_select_fusion.3), kind=kOutput, calls=%fused_computation.7 | convolution fusion | flops 100728832 | bytes 329728 | tf_op jit(solution)/shard_map/dot_general | solution.py:249
  56.7 1.3 %copy.9 = f32[4096,128]{1,0:T(8,128)} copy(f32[4096,128]{1,0:T(8,128)S(1)} %bitcast.30) | data formatting | bytes 4194304
  58.0 0.6 %copy.10 = f32[64,128]{1,0:T(8,128)} copy(f32[64,128]{1,0:T(8,128)S(1)} %get-tuple-element.21) | data formatting | bytes 65536
  (3 shorter events, 0.0 us)
Async XLA Ops:
  1.9 1.6 %copy-start = (f32[4096,128]{1,0:T(8,128)S(1)}, f32[4096,128]{1,0:T(8,128)}, u32[]{:S(2)}) copy-start(f32[4096,128]{1,0:T(8,128)} %param.5) | copy-start | bytes 6291460

commit v2 on v1

--- a/solution.py
+++ b/solution.py
@@ -68,6 +68,12 @@
     me_a, me_t = lax.axis_index("area"), lax.axis_index("tie")
     me = me_a * tie_n + me_t
 
+    blocks = 4 if devices % 4 == 0 else 1
+    block = devices // blocks
+    me_block, me_in = me // block, lax.rem(me, block)
+    upper = 2 * me_block >= blocks
+    turned = jnp.where(upper, me_block, blocks - 1 - me_block)
+
     def peer_of(k):
         peer = lax.rem(me + k, devices)
         return peer, (peer // tie_n, lax.rem(peer, tie_n))
@@ -93,17 +99,25 @@
         out_buf[phase] = value.reshape(devices, SLOT, snap)
         in_buf[phase, me] = out_buf[phase, me]
 
-        @pl.loop(1, devices)
-        def _(k):
-            peer, device = peer_of(k)
+        def post(peer):
             pltpu.make_async_remote_copy(
                 src_ref=out_buf.at[phase, peer],
                 dst_ref=in_buf.at[phase, me],
                 send_sem=send_sem.at[phase],
                 recv_sem=recv_sem.at[phase],
-                device_id=device,
+                device_id=(peer // tie_n, lax.rem(peer, tie_n)),
                 device_id_type=MESH,
             ).start()
+
+        @pl.loop(0, blocks - 1)
+        def _(b):
+            placed = b + jnp.where(b >= turned, 1, 0)
+            base = jnp.where(upper, placed, blocks - 1 - placed) * block
+            for i in range(block):
+                post(base + lax.rem(me_in + i, block))
+
+        for i in range(1, block):
+            post(me_block * block + lax.rem(me_in + i, block))
 
     def receive(phase):
         span = in_buf.at[phase, pl.ds(0, devices - 1)]

time: 58.8 us -> 56.8 us (0.966)
  Pallas kernels: 52.1 us -> 50.1 us
    pallas_call x1, Pallas kernels: 52.1 us -> 50.1 us  [on_device(): pl.pallas_call(functools.partial(kernel, area_n, tie_n), out_shape=(jax.S...]
where the time goes in v2:
time: 56.8 us; the launch traced here: 56.6 us
  Pallas kernels  50.1 us (88%)
  local copies, waits for them, and re-layouts  3.69 us (6%)
  matrix products  1.3 us (2%)
  other arithmetic  0.85 us (1%)
  between operations  0.67 us (1%)
    pallas_call x1, Pallas kernels, on_device(): pl.pallas_call(functools.partial(kernel, area_n, tie_n), out_shape=(jax.S...  50.1 us
    unnamed x4, local copies, waits for them, and re-layouts  3.53 us

profile of v2, /device:TPU:0, one launch (start us, length us, event | category | flops | bytes accessed | tf_op | source)
XLA Modules:
  0.0 56.6 jit_solution(10666070196102772151)
XLA Ops:
  0.6 0.7 %fusion.4 = (s32[512]{0:T(512)S(1)}, pred[512]{0:T(512)(128)(4,1)S(1)}, s32[512]{0:T(512)S(1)}, s32[512]{0:T(512)S(1)}) fusion(s32[4,128]{1,0:T(4,128)} %param.7, s32[4,128]{1,0:T(4,128)} %param.6), kind=kLoop, calls=%fused_computation.20 | loop fusion | flops 16896 | bytes 10752 | tf_op jit(solution)/shard_map/jit(_where)/select_n | solution.py:216
  1.3 0.3 fusion
  1.6 0.1 select_reduce_fusion
  1.8 0.1 broadcast_in_dim.59.srow_col
  1.9 0.1 broadcast_in_dim.62.svar_col
  1.9 0.0 copy-start
  1.9 1.6 %copy-done = f32[4096,128]{1,0:T(8,128)S(1)} copy-done((f32[4096,128]{1,0:T(8,128)S(1)}, f32[4096,128]{1,0:T(8,128)}, u32[]{:S(2)}) %copy-start) | copy-done | bytes 2097176
  3.5 50.1 %admm.1 = (f32[4,1024,128]{2,1,0:T(8,128)S(1)}, f32[64,128]{1,0:T(8,128)S(1)}, f32[128,128]{1,0:T(8,128)S(1)}) custom-call(s32[128,128]{1,0:T(8,128)S(1)} %broadcast_in_dim.59.srow_col, s32[8,128]{1,0:T(8,128)S(1)} %broadcast_in_dim.60.srow_lane, s32[128,128]{1,0:T(8,128)S(1)} %broadcast_in_dim.62.svar_col, bf16[4,1024,1024]{2,1,0:T(8,128)(2,1)} %g_hbm.1, ...), custom_call_target="tpu_custom_call" | custom-call | tf_op jit(solution)/shard_map/admm/pallas_call | solution.py:229
  53.7 1.0 %fusion.1 = f32[512,128]{1,0:T(8,128)} fusion(f32[128,128]{1,0:T(8,128)S(1)} %get-tuple-element.8, s32[512]{0:T(512)S(1)} %add_select_fusion.3), kind=kOutput, calls=%fused_computation.7 | convolution fusion | flops 100728832 | bytes 329728 | tf_op jit(solution)/shard_map/dot_general | solution.py:263
  54.7 1.3 %copy.9 = f32[4096,128]{1,0:T(8,128)} copy(f32[4096,128]{1,0:T(8,128)S(1)} %bitcast.30) | data formatting | bytes 4194304
  56.0 0.6 %copy.10 = f32[64,128]{1,0:T(8,128)} copy(f32[64,128]{1,0:T(8,128)S(1)} %get-tuple-element.21) | data formatting | bytes 65536
  (3 shorter events, 0.0 us)
Async XLA Ops:
  1.9 1.6 %copy-start = (f32[4096,128]{1,0:T(8,128)S(1)}, f32[4096,128]{1,0:T(8,128)}, u32[]{:S(2)}) copy-start(f32[4096,128]{1,0:T(8,128)} %param.5) | copy-start | bytes 6291460
